TPU v7x, 32 devices: a whole 2x2x4 slice. The times are simulated.
32 devices in a mesh: north: 8 (over z, x), deep: 4 (over y, core).
Axes of the slice: x: 2, y: 2, z: 4, core: 2. Of those that a mesh axis runs over, the one named last changes fastest.
Arguments:
- source: float32 [128, 128, 2048], P(None, 'north', 'deep'), may hold values from -6 to 6
- symbol_x: float32 [128], replicated, may hold values from 0.3 to 3
- symbol_y: float32 [128], replicated, may hold values from 0.3 to 3
- symbol_z: float32 [2048], replicated, may hold values from 0.3 to 3
Outputs:
- coefficients: float32 [64, 64, 1024], P('north', 'deep')
All inputs are finite; a program needn't handle non-finite values.
Results may differ from a plain program's by a relative error of at most 0.000071.
Values sent between devices are 32-bit elements; how exact they have to be, the bound alone decides.
A program may use at most 128 MiB of HBM per device.

v0:
```python
import functools

import jax
import jax.numpy as jnp
import numpy as np
from jax import lax
from jax.experimental import pallas as pl
from jax.experimental.pallas import tpu as pltpu
from jax.sharding import PartitionSpec as P

F32, BF16 = jnp.float32, jnp.bfloat16
FINE = 32
TILE = 256
SUB = 8
ROWS = 64


def angles(rows, modes, count):
    rank = np.outer(rows, modes) % (2 * count + 2)
    return np.pi / (count + 1) * rank


def split_np(table):
    high = table.astype(np.float32).astype(BF16)
    low = (table - high.astype(np.float64)).astype(np.float32).astype(BF16)
    return high, low


def left_table(count):
    gain = (2.0 / (count + 1)) ** 0.5
    table = np.sin(angles(np.arange(1, count // 2 + 1), np.arange(1, count + 1), count)) * gain
    return split_np(table)


def stacked(high, low):
    return np.block([[high, high], [low, np.zeros_like(low)]])


def long_tables(count):
    modes = np.arange(1, count // 2 + 1)
    gain = (2.0 / (count + 1)) ** 0.5
    coarse = angles(np.arange(0, count, FINE), modes, count)
    step = angles(np.arange(1, FINE + 1), modes, count)
    f32 = lambda v: jnp.asarray(v.astype(np.float32))
    return f32(np.sin(coarse) * gain), f32(np.cos(coarse) * gain), f32(np.sin(step)), f32(np.cos(step))


def split(values):
    high = values.astype(BF16)
    return high, (values - high.astype(F32)).astype(BF16)


def dot(a, b):
    return jnp.dot(a, b, preferred_element_type=F32)


def loop(count, body):
    if count == 1:
        body(0)
    else:
        lax.fori_loop(0, count, lambda i, c: (body(i), c)[1], 0)


def kernel(
    north, deep, each,
    src, tx, ty, sin_a, cos_a, sin_b, cos_b, symbol_x, symbol_y, symbol_z,
    out,
    field, turned, send1, recv1, send2, recv2, send3, recv3, t_high, t_low, left_all, left,
    fs, s1, r1, s2, r2, s3, r3,
):
    me_n, me_d = lax.axis_index("north"), lax.axis_index("deep")
    nx, ny_part, nz_part = src.shape
    halves = ny_part // SUB
    kept_z = t_high.shape[1]
    kept_y = ny_part * north // 2
    share_y = kept_y // deep
    half = north // 2
    pairs = deep // 2
    my_pair = me_d // 2
    far = jnp.where(me_n < half, half, 0)
    bases = (far, half - far)
    last = each - 1

    pieces = [(h, c) for h in range(halves) for c in range(0, nz_part, TILE)]
    loads = {}
    for i, (h, c) in enumerate(pieces):
        loads[h, c] = pltpu.make_async_copy(
            src.at[:, h * SUB : (h + 1) * SUB, c : c + TILE], field.at[h, :, :, c : c + TILE], fs.at[i]
        )
        loads[h, c].start()

    barrier = pltpu.get_barrier_semaphore()
    for r in range(1, deep):
        pl.semaphore_signal(barrier, inc=1, device_id={"deep": lax.rem(me_d + r, deep)})
    for r in range(1, north):
        pl.semaphore_signal(barrier, inc=1, device_id={"north": lax.rem(me_n + r, north)})

    def x_product(h, c):
        loads[h, c].wait()
        block = min(nx, 128)

        def turn(g):
            for k in range(0, block, 16):
                at = pl.multiple_of(g * block + k, 16)
                high, low = split(jnp.swapaxes(field[h, pl.ds(at, 16), :, c : c + TILE], 0, 1))
                turned[:, pl.ds(at, 16), :] = high
                turned[:, pl.ds(pl.multiple_of(nx + at, 16), 16), :] = low

        loop(nx // block, turn)
        rows = tx.shape[1] // 2
        group = rows // north

        def modes_of(g):
            modes = []
            for y in range(SUB):
                both = dot(tx[g], turned[y])
                modes.append(both[:rows] + both[rows:])
            for k in range(group):
                block = jnp.stack([m[k * north : (k + 1) * north] for m in modes])
                ed = g * group + k
                send1[ed // deep, lax.rem(ed, deep), h, :, :, c : c + TILE] = jnp.swapaxes(block, 0, 1)

        loop(tx.shape[0], modes_of)

    copies1 = {}

    def send_modes(f, e, h):
        for r in (*range(2, deep), 1):
            to = lax.bitwise_xor(me_d, r)
            at = pl.ds(bases[f], half)
            slot = (f * each + e) * halves + h
            copies1[f, e, h, r] = pltpu.make_async_remote_copy(
                src_ref=send1.at[e, to, h, at],
                dst_ref=recv1.at[e, me_d, h, at],
                send_sem=s1.at[slot, r],
                recv_sem=r1.at[slot, r],
                device_id={"deep": to},
            )
            copies1[f, e, h, r].start()

    chunks = [(f, e, h) for f in range(2) for e in range(each) for h in range(halves)]
    for h in range(halves):
        for c in range(0, nz_part, TILE):
            x_product(h, c)
        if h == 0:
            pl.semaphore_wait(barrier, deep + north - 2)
            send_modes(*chunks[0])
    for chunk in chunks[1:]:
        send_modes(*chunk)

    def table_step(a):
        table = sin_a[pl.ds(a, 1), :] * cos_b[...] + cos_a[pl.ds(a, 1), :] * sin_b[...]
        high, low = split(table)
        at = pl.multiple_of(a * FINE, FINE)
        t_high[pl.ds(at, FINE), :] = high
        t_low[pl.ds(at, FINE), :] = low

    loop(sin_a.shape[0], table_step)

    rows = half * SUB

    def z_product(lhs, count, pair):
        at = pl.multiple_of(pair * 2 * nz_part, 2 * nz_part)
        for c in range(0, kept_z, TILE):
            both = dot(lhs[...], t_high[pl.ds(at, 2 * nz_part), c : c + TILE])
            yield c, both[:count] + both[count:] + dot(
                lhs[:count, :], t_low[pl.ds(at, 2 * nz_part), c : c + TILE]
            )

    for chunk in chunks:
        copies1[(*chunk, 1)].wait_recv()
    total = rows * 2

    def near_part(k):
        e, h = k // halves, lax.rem(k, halves)
        for owner, block in ((me_d, send1), (lax.bitwise_xor(me_d, 1), recv1)):
            high, low = split(block[e, owner, h].reshape(total, nz_part))
            cols = pl.ds(pl.multiple_of(lax.rem(owner, 2) * nz_part, nz_part), nz_part)
            left_all[:total, cols] = high
            left_all[total:, cols] = low
        for c, value in z_product(left_all, total, my_pair):
            send2[e, h, :, :, c : c + TILE] = value.reshape(north, SUB, TILE)

    loop(each * halves, near_part)

    def inverse_roots():
        row = lax.broadcasted_iota(jnp.int32, (share_y, TILE), 0)
        part_y = jnp.zeros((share_y, TILE), F32)
        for j in range(share_y):
            part_y = jnp.where(row == j, symbol_y[me_d * share_y + j], part_y)
        for d in range(deep):
            for e in range(each):
                part_x = symbol_x[me_n * deep * each + d * each + e]
                for c in range(0, kept_z, TILE):
                    out[d, e, :, c : c + TILE] = lax.rsqrt(part_x + part_y + symbol_z[:, c : c + TILE])

    inverse_roots()

    def copy2(e, h, n):
        return pltpu.make_async_remote_copy(
            src_ref=send2.at[e, h, n],
            dst_ref=recv2.at[e, h, me_n],
            send_sem=s2.at[e * halves + h, n],
            recv_sem=r2.at[e * halves + h, me_n],
            device_id={"north": n},
        )

    def arrival2(e, h, n):
        return pltpu.make_async_remote_copy(
            src_ref=send2.at[e, h, n],
            dst_ref=recv2.at[e, h, n],
            send_sem=s2.at[e * halves + h, n],
            recv_sem=r2.at[e * halves + h, n],
            device_id={"north": n},
        )

    def others():
        for r in range(north - 1):
            yield r + (r >= me_n).astype(jnp.int32)

    copies3 = {}

    def y_stage(e, parts):
        for h in range(halves):
            for n in others():
                arrival2(e, h, n).wait_recv()
        width = kept_z // parts
        for p in range(parts):
            for c in range(p * width, (p + 1) * width, TILE):
                values = recv2[e, :, :, :, c : c + TILE].reshape(ny_part * north, TILE)
                both = dot(ty[...], jnp.concatenate(split(values), axis=0))
                modes = both[:kept_y] + both[kept_y:]
                send3[e, :, :, c : c + TILE] = modes.reshape(deep, share_y, TILE)
            cols = pl.ds(p * width, width)
            for r in (*range(2, deep), 1):
                to = lax.bitwise_xor(me_d, r)
                copies3[e, p, r] = pltpu.make_async_remote_copy(
                    src_ref=send3.at[e, to, :, cols],
                    dst_ref=recv3.at[me_d, e, :, cols],
                    send_sem=s3.at[e * 2 + p, r],
                    recv_sem=r3.at[e * 2 + p, r],
                    device_id={"deep": to},
                )
                copies3[e, p, r].start()

    for f, e, h in chunks:
        for pair in range(1, pairs):
            other = lax.rem(my_pair + pair, pairs)
            for k in range(2):
                owner = other * 2 + k
                r = lax.bitwise_xor(owner, me_d)
                slot = (f * each + e) * halves + h
                at = pl.ds(bases[f], half)
                pltpu.make_async_remote_copy(
                    src_ref=send1.at[e, owner, h, at],
                    dst_ref=recv1.at[e, owner, h, at],
                    send_sem=s1.at[slot, r],
                    recv_sem=r1.at[slot, r],
                    device_id={"deep": owner},
                ).wait_recv()
                high, low = split(recv1[e, owner, h, at].reshape(rows, nz_part))
                left[:rows, k * nz_part : (k + 1) * nz_part] = high
                left[rows:, k * nz_part : (k + 1) * nz_part] = low
            for c, value in z_product(left, rows, other):
                send2[e, h, at, :, c : c + TILE] += value.reshape(half, SUB, TILE)
        for i in range(half):
            n = bases[f] + i
            if f == 0:
                copy2(e, h, n).start()
            else:
                pl.when(n != me_n)(lambda: copy2(e, h, n).start())
        if f == 1:
            recv2[e, h, me_n] = send2[e, h, me_n]
            if h == halves - 1 and e < last:
                y_stage(e, 1)
    y_stage(last, 2)

    for copy in copies1.values():
        copy.wait_send()
    for e in range(each):
        for h in range(halves):
            for n in others():
                arrival2(e, h, n).wait_send()
    for e in range(each):
        out[me_d, e] = out[me_d, e] * send3[e, me_d]
        for p in range(2 if e == last else 1):
            for r in (1, *range(2, deep)):
                copy = copies3[e, p, r]
                copy.wait()
                width = kept_z // 2 if e == last else kept_z
                cols = slice(p * width, (p + 1) * width)
                owner = lax.bitwise_xor(me_d, r)
                out[owner, e, :, cols] = out[owner, e, :, cols] * recv3[owner, e, :, cols]


def on_device(source, symbol_x, symbol_y, symbol_z):
    north, deep = lax.axis_size("north"), lax.axis_size("deep")
    nx, ny_part, nz_part = source.shape
    each, halves = nx // 2 // north // deep, ny_part // SUB
    ny, nz = ny_part * north, nz_part * deep
    kept_z, share_y = nz // 2, ny // 2 // deep
    order = np.arange(nx // 2).reshape(north, deep, each).transpose(2, 1, 0).reshape(-1)
    x_high, x_low = left_table(nx)
    rows = max(ROWS, north)
    tx = jnp.asarray(np.stack([stacked(x_high[o], x_low[o]) for o in order.reshape(-1, rows)]))
    order = np.arange(ny).reshape(north, halves, SUB).transpose(1, 0, 2).reshape(-1)
    y_high, y_low = left_table(ny)
    ty = jnp.asarray(stacked(y_high[:, order], y_low[:, order]))
    vmem = pl.BlockSpec(memory_space=pltpu.VMEM)
    smem = pl.BlockSpec(memory_space=pltpu.SMEM)
    chunks = each * halves
    rows = SUB * north
    v = pl.pallas_call(
        functools.partial(kernel, north, deep, each),
        out_shape=jax.ShapeDtypeStruct((deep, each, share_y, kept_z), F32),
        in_specs=[pl.BlockSpec(memory_space=pl.ANY)] + [vmem] * 6 + [smem] * 2 + [vmem],
        out_specs=vmem,
        scratch_shapes=[
            pltpu.VMEM((halves, nx, SUB, nz_part), F32),
            pltpu.VMEM((SUB, 2 * nx, TILE), BF16),
            pltpu.VMEM((each, deep, halves, north, SUB, nz_part), F32),
            pltpu.VMEM((each, deep, halves, north, SUB, nz_part), F32),
            pltpu.VMEM((each, halves, north, SUB, kept_z), F32),
            pltpu.VMEM((each, halves, north, SUB, kept_z), F32),
            pltpu.VMEM((each, deep, share_y, kept_z), F32),
            pltpu.VMEM((deep, each, share_y, kept_z), F32),
            pltpu.VMEM((nz, kept_z), BF16),
            pltpu.VMEM((nz, kept_z), BF16),
            pltpu.VMEM((2 * rows, 2 * nz_part), BF16),
            pltpu.VMEM((rows, 2 * nz_part), BF16),
            pltpu.SemaphoreType.DMA((halves * nz_part // TILE,)),
        ]
        + [
            pltpu.SemaphoreType.DMA((sets, peers))
            for sets, peers in ((2 * chunks, deep), (chunks, north), (2 * each, deep))
            for _ in range(2)
        ],
        compiler_params=pltpu.CompilerParams(
            collective_id=0, has_side_effects=True, vmem_limit_bytes=67043328
        ),
    )(source, tx, ty, *long_tables(nz), symbol_x, symbol_y, symbol_z[None, :])
    return v.reshape(deep * each, share_y, kept_z)


def solution(mesh):
    in_specs = (P(None, "north", "deep"), P(), P(), P())
    out_specs = P("north", "deep", None)
    return jax.shard_map(
        on_device, mesh=mesh, in_specs=in_specs, out_specs=out_specs, check_vma=False
    )
```

profile of v0, /device:TPU:0, one launch (start us, length us, event | category | flops | bytes accessed | tf_op | source)
XLA Modules:
  0.0 48.2 jit_solution(7992353938468986017)
XLA Ops:
  0.0 46.3 %shard_map.100 = f32[4,2,16,1024]{3,2,1,0:T(8,128)} custom-call(f32[128,16,512]{2,1,0:T(8,128)} %src.1, bf16[1,128,256]{2,1,0:T(8,128)(2,1)} %constant.12.clone.tx, bf16[128,256]{1,0:T(8,128)(2,1)} %constant.13.clone.ty, f32[64,1024]{1,0:T(8,128)} %constant.14.clone.sin_a, f32[64,1024]{1,0:T(8,128)} %constant.15.clone.cos_a, ...), custom_call_target="tpu_custom_call" | custom-call | tf_op jit(solution)/shard_map/pallas_call | solution.py:313
  46.3 1.9 %copy.12 = f32[8,16,1024]{2,1,0:T(8,128)} copy(f32[8,16,1024]{2,1,0:T(8,128)} %bitcast.2) | data formatting | bytes 1048576
where the time goes:
time: 48.3 us; the launch traced here: 48.2 us
  Pallas kernels  46.3 us (96%)
  local copies, waits for them, and re-layouts  1.89 us (4%)
    pallas_call x1, Pallas kernels, on_device(): pl.pallas_call(functools.partial(kernel, north, deep, each), out_shape=ja...  46.3 us
    unnamed x1, local copies, waits for them, and re-layouts  1.89 us

commit v1 on v0

v1 whole, which is shorter than its diff:
```python
import functools

import jax
import jax.numpy as jnp
import numpy as np
from jax import lax
from jax.experimental import pallas as pl
from jax.experimental.pallas import tpu as pltpu
from jax.sharding import PartitionSpec as P

F32, BF16 = jnp.float32, jnp.bfloat16
FINE = 32
TILE = 256
SUB = 8
ROWS = 64


def angles(rows, modes, count):
    rank = np.outer(rows, modes) % (2 * count + 2)
    return np.pi / (count + 1) * rank


def split_np(table):
    high = table.astype(np.float32).astype(BF16)
    low = (table - high.astype(np.float64)).astype(np.float32).astype(BF16)
    return high, low


def left_table(count):
    gain = (2.0 / (count + 1)) ** 0.5
    table = np.sin(angles(np.arange(1, count // 2 + 1), np.arange(1, count + 1), count)) * gain
    return split_np(table)


def stacked(high, low):
    return np.block([[high, high], [low, np.zeros_like(low)]])


def long_tables(count):
    modes = np.arange(1, count // 2 + 1)
    gain = (2.0 / (count + 1)) ** 0.5
    coarse = angles(np.arange(0, count, FINE), modes, count)
    step = angles(np.arange(1, FINE + 1), modes, count)
    f32 = lambda v: jnp.asarray(v.astype(np.float32))
    return f32(np.sin(coarse) * gain), f32(np.cos(coarse) * gain), f32(np.sin(step)), f32(np.cos(step))


def split(values):
    high = values.astype(BF16)
    return high, (values - high.astype(F32)).astype(BF16)


def dot(a, b):
    return jnp.dot(a, b, preferred_element_type=F32)


def loop(count, body):
    if count == 1:
        body(0)
    else:
        lax.fori_loop(0, count, lambda i, c: (body(i), c)[1], 0)


def kernel(
    north, deep, each,
    src, tx_in, ty_in, *rest,
):
    tables_in, (sx_in, sy_in, sz_in, out), scratch = rest[:4], rest[4:8], rest[8:]
    tx, ty, sin_a, cos_a, sin_b, cos_b, symbol_x, symbol_y, symbol_z = scratch[:9]
    field, turned, send1, recv1, send2, recv2, send3, recv3, t_high, t_low, left_all, left = scratch[9:21]
    fs, ins, s1, r1, s2, r2, s3, r3 = scratch[21:]

    me_n, me_d = lax.axis_index("north"), lax.axis_index("deep")
    nx, ny_part, nz_part = src.shape
    halves = ny_part // SUB
    kept_z = t_high.shape[1]
    kept_y = ny_part * north // 2
    share_y = kept_y // deep
    half = north // 2
    pairs = deep // 2
    my_pair = me_d // 2
    far = jnp.where(me_n < half, half, 0)
    bases = (far, half - far)
    last = each - 1
    parts = kept_z // TILE

    loads = {}
    small = []

    def fetch(what, to):
        copy = pltpu.make_async_copy(what, to, ins.at[len(small)])
        copy.start()
        small.append(copy)

    fetch(tx_in, tx)
    for i, (h, c) in enumerate((h, c) for h in range(halves) for c in range(0, nz_part, TILE)):
        loads[h, c] = pltpu.make_async_copy(
            src.at[:, h * SUB : (h + 1) * SUB, c : c + TILE], field.at[h, :, :, c : c + TILE], fs.at[i]
        )
        loads[h, c].start()
    for what, to in zip(
        (*tables_in, ty_in, sx_in, sy_in, sz_in),
        (sin_a, cos_a, sin_b, cos_b, ty, symbol_x, symbol_y, symbol_z),
    ):
        fetch(what, to)

    barrier = pltpu.get_barrier_semaphore()
    for r in range(1, deep):
        pl.semaphore_signal(barrier, inc=1, device_id={"deep": lax.rem(me_d + r, deep)})
    for r in range(1, north):
        pl.semaphore_signal(barrier, inc=1, device_id={"north": lax.rem(me_n + r, north)})

    def x_product(h, c):
        loads[h, c].wait()
        block = min(nx, 128)

        def turn(g):
            for k in range(0, block, 16):
                at = pl.multiple_of(g * block + k, 16)
                high, low = split(jnp.swapaxes(field[h, pl.ds(at, 16), :, c : c + TILE], 0, 1))
                turned[:, pl.ds(at, 16), :] = high
                turned[:, pl.ds(pl.multiple_of(nx + at, 16), 16), :] = low

        loop(nx // block, turn)
        rows = tx.shape[1] // 2
        group = rows // north

        def modes_of(g):
            modes = []
            for y in range(SUB):
                both = dot(tx[g], turned[y])
                modes.append(both[:rows] + both[rows:])
            for k in range(group):
                block = jnp.stack([m[k * north : (k + 1) * north] for m in modes])
                ed = g * group + k
                send1[ed // deep, lax.rem(ed, deep), h, :, :, c : c + TILE] = jnp.swapaxes(block, 0, 1)

        loop(tx.shape[0], modes_of)

    chunks = []
    for f in range(2):
        for e in range(each):
            for h in range(halves):
                cut = half // 2 if not chunks and half % 2 == 0 else half
                chunks += [(f, e, h, i, cut) for i in range(0, half, cut)]

    def copy1(q, r, source):
        f, e, h, i, count = chunks[q]
        at = pl.ds(bases[f] + i, count)
        to = lax.bitwise_xor(me_d, r)
        return pltpu.make_async_remote_copy(
            src_ref=send1.at[e, to, h, at],
            dst_ref=recv1.at[e, source, h, at],
            send_sem=s1.at[q, r],
            recv_sem=r1.at[q, r],
            device_id={"deep": to},
        )

    def send_modes(h_done):
        for q, chunk in enumerate(chunks):
            if (q < half // chunks[0][4]) == (h_done == 0):
                for r in (*range(2, deep), 1):
                    copy1(q, r, me_d).start()

    for h in range(halves):
        for c in range(0, nz_part, TILE):
            if (h, c) == (0, 0):
                small[0].wait()
            x_product(h, c)
        if h == 0:
            pl.semaphore_wait(barrier, deep + north - 2)
            send_modes(0)
    send_modes(1)

    for copy in small[1:]:
        copy.wait()

    def table_step(a):
        table = sin_a[pl.ds(a, 1), :] * cos_b[...] + cos_a[pl.ds(a, 1), :] * sin_b[...]
        high, low = split(table)
        at = pl.multiple_of(a * FINE, FINE)
        t_high[pl.ds(at, FINE), :] = high
        t_low[pl.ds(at, FINE), :] = low

    loop(sin_a.shape[0], table_step)

    def z_product(lhs, count, pair):
        at = pl.multiple_of(pair * 2 * nz_part, 2 * nz_part)
        for c in range(0, kept_z, TILE):
            both = dot(lhs[: 2 * count], t_high[pl.ds(at, 2 * nz_part), c : c + TILE])
            yield c, both[:count] + both[count:] + dot(
                lhs[:count], t_low[pl.ds(at, 2 * nz_part), c : c + TILE]
            )

    def near_part(f, e):
        for q, chunk in enumerate(chunks):
            if chunk[:2] == (f, e):
                copy1(q, 1, lax.bitwise_xor(me_d, 1)).wait_recv()
        at = pl.ds(bases[f], half)
        count = halves * half * SUB
        for owner, block in ((me_d, send1), (lax.bitwise_xor(me_d, 1), recv1)):
            high, low = split(block[e, owner, :, at].reshape(count, nz_part))
            cols = pl.ds(pl.multiple_of(lax.rem(owner, 2) * nz_part, nz_part), nz_part)
            left_all[:count, cols] = high
            left_all[count:, cols] = low
        for c, value in z_product(left_all, count, my_pair):
            value = value.reshape(halves, half, SUB, TILE)
            for h in range(halves):
                send2[e, at, h * SUB : (h + 1) * SUB, c : c + TILE] = value[h]

    def inverse_roots():
        row = lax.broadcasted_iota(jnp.int32, (share_y, TILE), 0)
        part_y = jnp.zeros((share_y, TILE), F32)
        for j in range(share_y):
            part_y = jnp.where(row == j, symbol_y[me_d * share_y + j], part_y)
        for d in range(deep):
            for e in range(each):
                part_x = symbol_x[me_n * deep * each + d * each + e]
                for c in range(0, kept_z, TILE):
                    out[d, e, :, c : c + TILE] = lax.rsqrt(part_x + part_y + symbol_z[:, c : c + TILE])

    def units(e):
        return parts if e == last else halves

    def copy2(e, u, n, source):
        rows = slice(None) if e == last else slice(u * SUB, (u + 1) * SUB)
        cols = slice(u * TILE, (u + 1) * TILE) if e == last else slice(None)
        base = e * halves
        return pltpu.make_async_remote_copy(
            src_ref=send2.at[e, n, rows, cols],
            dst_ref=recv2.at[e, source, rows, cols],
            send_sem=s2.at[base + u, n],
            recv_sem=r2.at[base + u, source],
            device_id={"north": n},
        )

    def every(count, body):
        if count <= 8:
            for i in range(count):
                body(i)
        else:
            loop(count, body)

    def send_north(f, e, u, i, count):
        def one(k):
            n = bases[f] + i + k
            if f == 0:
                copy2(e, u, n, me_n).start()
            else:
                pl.when(n != me_n)(lambda: copy2(e, u, n, me_n).start())

        every(count, one)

    def others(body):
        every(north - 1, lambda r: body(r + jnp.asarray(r >= me_n, jnp.int32)))

    def copy3(e, p, r, owner):
        to = lax.bitwise_xor(me_d, r)
        cols = slice(p * TILE, (p + 1) * TILE) if e == last else slice(None)
        return pltpu.make_async_remote_copy(
            src_ref=send3.at[e, to, :, cols],
            dst_ref=recv3.at[owner, e, :, cols],
            send_sem=s3.at[e + p, r],
            recv_sem=r3.at[e + p, r],
            device_id={"deep": to},
        )

    def y_stage(e, p):
        for u in range(halves) if e < last else (p,):
            others(lambda n: copy2(e, u, n, n).wait_recv())
        for c in range(0, kept_z, TILE) if e < last else (p * TILE,):
            values = recv2[e, :, :, c : c + TILE].reshape(ny_part * north, TILE)
            both = dot(ty[...], jnp.concatenate(split(values), axis=0))
            modes = both[:kept_y] + both[kept_y:]
            send3[e, :, :, c : c + TILE] = modes.reshape(deep, share_y, TILE)
        for r in (*range(2, deep), 1):
            copy3(e, p, r, me_d).start()

    for q, (f, e, h, i, count) in enumerate(chunks):
        if h == 0 and i == 0:
            near_part(f, e)
        rows = count * SUB
        at = pl.ds(bases[f] + i, count)
        for pair in range(1, pairs):
            other = lax.rem(my_pair + pair, pairs)
            for k in range(2):
                owner = other * 2 + k
                r = lax.bitwise_xor(owner, me_d)
                copy1(q, r, owner).wait_recv()
                high, low = split(recv1[e, owner, h, at].reshape(rows, nz_part))
                left[:rows, k * nz_part : (k + 1) * nz_part] = high
                left[rows : 2 * rows, k * nz_part : (k + 1) * nz_part] = low
            for c, value in z_product(left, rows, other):
                send2[e, at, h * SUB : (h + 1) * SUB, c : c + TILE] += value.reshape(count, SUB, TILE)
        if e < last:
            send_north(f, e, h, i, count)
        elif h == halves - 1:
            for u in range(parts):
                send_north(f, e, u, 0, half)
        if q == 0:
            inverse_roots()

    for e in range(each):
        recv2[e, me_n] = send2[e, me_n]
    for e in range(each):
        for p in range(parts if e == last else 1):
            y_stage(e, p)

    for q in range(len(chunks)):
        for r in range(1, deep):
            copy1(q, r, me_d).wait_send()
    for e in range(each):
        for u in range(units(e)):
            others(lambda n: copy2(e, u, n, me_n).wait_send())
    for e in range(each):
        out[me_d, e] = out[me_d, e] * send3[e, me_d]
        for p in range(parts if e == last else 1):
            cols = slice(p * TILE, (p + 1) * TILE) if e == last else slice(None)
            for r in range(1, deep):
                owner = lax.bitwise_xor(me_d, r)
                copy = copy3(e, p, r, owner)
                copy.wait_recv()
                out[owner, e, :, cols] = out[owner, e, :, cols] * recv3[owner, e, :, cols]
                copy.wait_send()


def on_device(source, symbol_x, symbol_y, symbol_z):
    north, deep = lax.axis_size("north"), lax.axis_size("deep")
    nx, ny_part, nz_part = source.shape
    each, halves = nx // 2 // north // deep, ny_part // SUB
    ny, nz = ny_part * north, nz_part * deep
    kept_z, share_y = nz // 2, ny // 2 // deep
    order = np.arange(nx // 2).reshape(north, deep, each).transpose(2, 1, 0).reshape(-1)
    x_high, x_low = left_table(nx)
    rows = max(ROWS, north)
    tx = jnp.asarray(np.stack([stacked(x_high[o], x_low[o]) for o in order.reshape(-1, rows)]))
    ty = jnp.asarray(stacked(*left_table(ny)))
    tables = long_tables(nz)
    anywhere = pl.BlockSpec(memory_space=pl.ANY)
    rows = SUB * north
    chunks = 2 * each * halves + 1
    operands = (source, tx, ty, *tables, symbol_x, symbol_y, symbol_z[None, :])
    v = pl.pallas_call(
        functools.partial(kernel, north, deep, each),
        out_shape=jax.ShapeDtypeStruct((deep, each, share_y, kept_z), F32),
        in_specs=[anywhere] * len(operands),
        out_specs=pl.BlockSpec(memory_space=pltpu.VMEM),
        scratch_shapes=[pltpu.VMEM(t.shape, t.dtype) for t in (tx, ty, *tables)]
        + [
            pltpu.SMEM(symbol_x.shape, F32),
            pltpu.SMEM(symbol_y.shape, F32),
            pltpu.VMEM((1, nz), F32),
            pltpu.VMEM((halves, nx, SUB, nz_part), F32),
            pltpu.VMEM((SUB, 2 * nx, TILE), BF16),
            pltpu.VMEM((each, deep, halves, north, SUB, nz_part), F32),
            pltpu.VMEM((each, deep, halves, north, SUB, nz_part), F32),
            pltpu.VMEM((each, north, ny_part, kept_z), F32),
            pltpu.VMEM((each, north, ny_part, kept_z), F32),
            pltpu.VMEM((each, deep, share_y, kept_z), F32),
            pltpu.VMEM((deep, each, share_y, kept_z), F32),
            pltpu.VMEM((nz, kept_z), BF16),
            pltpu.VMEM((nz, kept_z), BF16),
            pltpu.VMEM((halves * rows, 2 * nz_part), BF16),
            pltpu.VMEM((rows, 2 * nz_part), BF16),
            pltpu.SemaphoreType.DMA((halves * nz_part // TILE,)),
            pltpu.SemaphoreType.DMA((len(operands),)),
        ]
        + [
            pltpu.SemaphoreType.DMA((sets, peers))
            for sets, peers in (
                (chunks, deep),
                (each * halves + kept_z // TILE, north),
                (each + kept_z // TILE, deep),
            )
            for _ in range(2)
        ],
        compiler_params=pltpu.CompilerParams(
            collective_id=0, has_side_effects=True, vmem_limit_bytes=67043328
        ),
    )(*operands)
    return v.reshape(deep * each, share_y, kept_z)


def solution(mesh):
    in_specs = (P(None, "north", "deep"), P(), P(), P())
    out_specs = P("north", "deep", None)
    return jax.shard_map(
        on_device, mesh=mesh, in_specs=in_specs, out_specs=out_specs, check_vma=False
    )
```

time: 48.3 us -> 44.7 us (0.925)
  Pallas kernels: 46.3 us -> 42.6 us
    pallas_call x1, Pallas kernels: 46.3 us -> 42.6 us  [on_device(): pl.pallas_call(functools.partial(kernel, north, deep, each), out_shape=ja...]
where the time goes in v1:
time: 44.7 us; the launch traced here: 44.5 us
  Pallas kernels  42.6 us (95%)
  local copies, waits for them, and re-layouts  1.89 us (4%)
    pallas_call x1, Pallas kernels, on_device(): pl.pallas_call(functools.partial(kernel, north, deep, each), out_shape=ja...  42.6 us
    unnamed x1, local copies, waits for them, and re-layouts  1.89 us

profile of v1, /device:TPU:0, one launch (start us, length us, event | category | flops | bytes accessed | tf_op | source)
XLA Modules:
  0.0 44.5 jit_solution(2923229256683912028)
XLA Ops:
  0.0 42.6 %shard_map.100 = f32[4,2,16,1024]{3,2,1,0:T(8,128)} custom-call(f32[128,16,512]{2,1,0:T(8,128)} %src.1, bf16[1,128,256]{2,1,0:T(8,128)(2,1)} %constant.12.clone.tx_in, bf16[128,256]{1,0:T(8,128)(2,1)} %constant.13.clone.ty_in, f32[64,1024]{1,0:T(8,128)} %constant.14.clone.rest_0_, f32[64,1024]{1,0:T(8,128)} %constant.15.clone.rest_1_, ...), custom_call_target="tpu_custom_call" | custom-call | tf_op jit(solution)/shard_map/pallas_call | solution.py:343
  42.7 1.9 %copy.12 = f32[8,16,1024]{2,1,0:T(8,128)} copy(f32[8,16,1024]{2,1,0:T(8,128)} %bitcast.2) | data formatting | bytes 1048576

commit v2 on v1

--- a/solution.py
+++ b/solution.py
@@ -41,8 +41,8 @@
     gain = (2.0 / (count + 1)) ** 0.5
     coarse = angles(np.arange(0, count, FINE), modes, count)
     step = angles(np.arange(1, FINE + 1), modes, count)
-    f32 = lambda v: jnp.asarray(v.astype(np.float32))
-    return f32(np.sin(coarse) * gain), f32(np.cos(coarse) * gain), f32(np.sin(step)), f32(np.cos(step))
+    parts = (np.sin(coarse) * gain, np.cos(coarse) * gain, np.sin(step), np.cos(step))
+    return jnp.asarray(np.concatenate(parts).astype(np.float32))
 
 
 def split(values):
@@ -65,10 +65,10 @@
     north, deep, each,
     src, tx_in, ty_in, *rest,
 ):
-    tables_in, (sx_in, sy_in, sz_in, out), scratch = rest[:4], rest[4:8], rest[8:]
-    tx, ty, sin_a, cos_a, sin_b, cos_b, symbol_x, symbol_y, symbol_z = scratch[:9]
-    field, turned, send1, recv1, send2, recv2, send3, recv3, t_high, t_low, left_all, left = scratch[9:21]
-    fs, ins, s1, r1, s2, r2, s3, r3 = scratch[21:]
+    waves_in, sx_in, sy_in, sz_in, out = rest[:5]
+    tx, ty, waves, symbol_x, symbol_y, symbol_z = rest[5:11]
+    field, turned, send1, recv1, send2, recv2, send3, recv3, t_high, t_low, left_all, left = rest[11:23]
+    fs, ins, sent, r1, r2, r3 = rest[23:]
 
     me_n, me_d = lax.axis_index("north"), lax.axis_index("deep")
     nx, ny_part, nz_part = src.shape
@@ -99,8 +99,8 @@
         )
         loads[h, c].start()
     for what, to in zip(
-        (*tables_in, ty_in, sx_in, sy_in, sz_in),
-        (sin_a, cos_a, sin_b, cos_b, ty, symbol_x, symbol_y, symbol_z),
+        (waves_in, ty_in, sx_in, sy_in, sz_in),
+        (waves, ty, symbol_x, symbol_y, symbol_z),
     ):
         fetch(what, to)
 
@@ -144,15 +144,16 @@
                 cut = half // 2 if not chunks and half % 2 == 0 else half
                 chunks += [(f, e, h, i, cut) for i in range(0, half, cut)]
 
-    def copy1(q, r, source):
+    def copy1(q, r):
         f, e, h, i, count = chunks[q]
         at = pl.ds(bases[f] + i, count)
         to = lax.bitwise_xor(me_d, r)
+        key = 2 * each * halves + 1 + f * each + e if r == 1 else q
         return pltpu.make_async_remote_copy(
             src_ref=send1.at[e, to, h, at],
-            dst_ref=recv1.at[e, source, h, at],
-            send_sem=s1.at[q, r],
-            recv_sem=r1.at[q, r],
+            dst_ref=recv1.at[e, me_d, h, at],
+            send_sem=sent.at[0],
+            recv_sem=r1.at[key],
             device_id={"deep": to},
         )
 
@@ -160,7 +161,7 @@
         for q, chunk in enumerate(chunks):
             if (q < half // chunks[0][4]) == (h_done == 0):
                 for r in (*range(2, deep), 1):
-                    copy1(q, r, me_d).start()
+                    copy1(q, r).start()
 
     for h in range(halves):
         for c in range(0, nz_part, TILE):
@@ -175,14 +176,17 @@
     for copy in small[1:]:
         copy.wait()
 
+    coarse = waves.shape[0] // 2 - FINE
+
     def table_step(a):
-        table = sin_a[pl.ds(a, 1), :] * cos_b[...] + cos_a[pl.ds(a, 1), :] * sin_b[...]
+        sin_a, cos_a = waves[pl.ds(a, 1), :], waves[pl.ds(coarse + a, 1), :]
+        table = sin_a * waves[2 * coarse + FINE :, :] + cos_a * waves[2 * coarse : 2 * coarse + FINE, :]
         high, low = split(table)
         at = pl.multiple_of(a * FINE, FINE)
         t_high[pl.ds(at, FINE), :] = high
         t_low[pl.ds(at, FINE), :] = low
 
-    loop(sin_a.shape[0], table_step)
+    loop(coarse, table_step)
 
     def z_product(lhs, count, pair):
         at = pl.multiple_of(pair * 2 * nz_part, 2 * nz_part)
@@ -193,10 +197,9 @@
             )
 
     def near_part(f, e):
-        for q, chunk in enumerate(chunks):
-            if chunk[:2] == (f, e):
-                copy1(q, 1, lax.bitwise_xor(me_d, 1)).wait_recv()
         at = pl.ds(bases[f], half)
+        block = recv1.at[e, lax.bitwise_xor(me_d, 1), :, at]
+        pltpu.make_async_copy(block, block, r1.at[2 * each * halves + 1 + f * each + e]).wait()
         count = halves * half * SUB
         for owner, block in ((me_d, send1), (lax.bitwise_xor(me_d, 1), recv1)):
             high, low = split(block[e, owner, :, at].reshape(count, nz_part))
@@ -222,15 +225,14 @@
     def units(e):
         return parts if e == last else halves
 
-    def copy2(e, u, n, source):
+    def copy2(e, u, n):
         rows = slice(None) if e == last else slice(u * SUB, (u + 1) * SUB)
         cols = slice(u * TILE, (u + 1) * TILE) if e == last else slice(None)
-        base = e * halves
         return pltpu.make_async_remote_copy(
             src_ref=send2.at[e, n, rows, cols],
-            dst_ref=recv2.at[e, source, rows, cols],
-            send_sem=s2.at[base + u, n],
-            recv_sem=r2.at[base + u, source],
+            dst_ref=recv2.at[e, me_n, rows, cols],
+            send_sem=sent.at[1],
+            recv_sem=r2.at[e + u if e == last else e],
             device_id={"north": n},
         )
 
@@ -245,36 +247,34 @@
         def one(k):
             n = bases[f] + i + k
             if f == 0:
-                copy2(e, u, n, me_n).start()
+                copy2(e, u, n).start()
             else:
-                pl.when(n != me_n)(lambda: copy2(e, u, n, me_n).start())
+                pl.when(n != me_n)(lambda: copy2(e, u, n).start())
 
         every(count, one)
 
-    def others(body):
-        every(north - 1, lambda r: body(r + jnp.asarray(r >= me_n, jnp.int32)))
-
-    def copy3(e, p, r, owner):
+    def copy3(e, p, r):
         to = lax.bitwise_xor(me_d, r)
         cols = slice(p * TILE, (p + 1) * TILE) if e == last else slice(None)
         return pltpu.make_async_remote_copy(
             src_ref=send3.at[e, to, :, cols],
-            dst_ref=recv3.at[owner, e, :, cols],
-            send_sem=s3.at[e + p, r],
-            recv_sem=r3.at[e + p, r],
+            dst_ref=recv3.at[me_d, e, :, cols],
+            send_sem=sent.at[2],
+            recv_sem=r3.at[e + p],
             device_id={"deep": to},
         )
 
     def y_stage(e, p):
-        for u in range(halves) if e < last else (p,):
-            others(lambda n: copy2(e, u, n, n).wait_recv())
+        cols = slice(p * TILE, (p + 1) * TILE) if e == last else slice(None)
+        block = recv2.at[e, pl.ds(0, north - 1), :, cols]
+        pltpu.make_async_copy(block, block, r2.at[e + p]).wait()
         for c in range(0, kept_z, TILE) if e < last else (p * TILE,):
             values = recv2[e, :, :, c : c + TILE].reshape(ny_part * north, TILE)
             both = dot(ty[...], jnp.concatenate(split(values), axis=0))
             modes = both[:kept_y] + both[kept_y:]
             send3[e, :, :, c : c + TILE] = modes.reshape(deep, share_y, TILE)
         for r in (*range(2, deep), 1):
-            copy3(e, p, r, me_d).start()
+            copy3(e, p, r).start()
 
     for q, (f, e, h, i, count) in enumerate(chunks):
         if h == 0 and i == 0:
@@ -283,10 +283,10 @@
         at = pl.ds(bases[f] + i, count)
         for pair in range(1, pairs):
             other = lax.rem(my_pair + pair, pairs)
+            block = recv1.at[e, pl.ds(other * 2, 2), h, at]
+            pltpu.make_async_copy(block, block, r1.at[q]).wait()
             for k in range(2):
                 owner = other * 2 + k
-                r = lax.bitwise_xor(owner, me_d)
-                copy1(q, r, owner).wait_recv()
                 high, low = split(recv1[e, owner, h, at].reshape(rows, nz_part))
                 left[:rows, k * nz_part : (k + 1) * nz_part] = high
                 left[rows : 2 * rows, k * nz_part : (k + 1) * nz_part] = low
@@ -306,22 +306,21 @@
         for p in range(parts if e == last else 1):
             y_stage(e, p)
 
-    for q in range(len(chunks)):
-        for r in range(1, deep):
-            copy1(q, r, me_d).wait_send()
-    for e in range(each):
-        for u in range(units(e)):
-            others(lambda n: copy2(e, u, n, me_n).wait_send())
     for e in range(each):
         out[me_d, e] = out[me_d, e] * send3[e, me_d]
         for p in range(parts if e == last else 1):
             cols = slice(p * TILE, (p + 1) * TILE) if e == last else slice(None)
+            block = recv3.at[pl.ds(0, deep - 1), e, :, cols]
+            pltpu.make_async_copy(block, block, r3.at[e + p]).wait()
             for r in range(1, deep):
                 owner = lax.bitwise_xor(me_d, r)
-                copy = copy3(e, p, r, owner)
-                copy.wait_recv()
                 out[owner, e, :, cols] = out[owner, e, :, cols] * recv3[owner, e, :, cols]
-                copy.wait_send()
+    for i, block in enumerate((
+        send1.at[:, pl.ds(0, deep - 1)],
+        send2.at[:, pl.ds(0, north - 1)],
+        send3.at[:, pl.ds(0, deep - 1)],
+    )):
+        pltpu.make_async_copy(block, block, sent.at[i]).wait()
 
 
 def on_device(source, symbol_x, symbol_y, symbol_z):
@@ -335,17 +334,17 @@
     rows = max(ROWS, north)
     tx = jnp.asarray(np.stack([stacked(x_high[o], x_low[o]) for o in order.reshape(-1, rows)]))
     ty = jnp.asarray(stacked(*left_table(ny)))
-    tables = long_tables(nz)
-    anywhere = pl.BlockSpec(memory_space=pl.ANY)
+    waves = long_tables(nz)
+    remote = pl.BlockSpec(memory_space=pltpu.HBM)
     rows = SUB * north
     chunks = 2 * each * halves + 1
-    operands = (source, tx, ty, *tables, symbol_x, symbol_y, symbol_z[None, :])
+    operands = (source, tx, ty, waves, symbol_x, symbol_y, symbol_z[None, :])
     v = pl.pallas_call(
         functools.partial(kernel, north, deep, each),
         out_shape=jax.ShapeDtypeStruct((deep, each, share_y, kept_z), F32),
-        in_specs=[anywhere] * len(operands),
+        in_specs=[remote] * len(operands),
         out_specs=pl.BlockSpec(memory_space=pltpu.VMEM),
-        scratch_shapes=[pltpu.VMEM(t.shape, t.dtype) for t in (tx, ty, *tables)]
+        scratch_shapes=[pltpu.VMEM(t.shape, t.dtype) for t in (tx, ty, waves)]
         + [
             pltpu.SMEM(symbol_x.shape, F32),
             pltpu.SMEM(symbol_y.shape, F32),
@@ -363,16 +362,11 @@
             pltpu.VMEM((halves * rows, 2 * nz_part), BF16),
             pltpu.VMEM((rows, 2 * nz_part), BF16),
             pltpu.SemaphoreType.DMA((halves * nz_part // TILE,)),
-            pltpu.SemaphoreType.DMA((len(operands),)),
+            pltpu.SemaphoreType.DMA((len(operands) - 1,)),
         ]
         + [
-            pltpu.SemaphoreType.DMA((sets, peers))
-            for sets, peers in (
-                (chunks, deep),
-                (each * halves + kept_z // TILE, north),
-                (each + kept_z // TILE, deep),
-            )
-            for _ in range(2)
+            pltpu.SemaphoreType.DMA((count,))
+            for count in (3, chunks + 2 * each, each + kept_z // TILE, each + kept_z // TILE)
         ],
         compiler_params=pltpu.CompilerParams(
             collective_id=0, has_side_effects=True, vmem_limit_bytes=67043328

time: 44.7 us -> 42.7 us (0.955)
  Pallas kernels: 42.6 us -> 40.7 us
    pallas_call x1, Pallas kernels: 42.6 us -> 40.7 us  [on_device(): pl.pallas_call(functools.partial(kernel, north, deep, each), out_shape=ja...]
where the time goes in v2:
time: 42.7 us; the launch traced here: 42.5 us
  Pallas kernels  40.7 us (95%)
  local copies, waits for them, and re-layouts  1.89 us (4%)
    pallas_call x1, Pallas kernels, on_device(): pl.pallas_call(functools.partial(kernel, north, deep, each), out_shape=ja...  40.7 us
    unnamed x1, local copies, waits for them, and re-layouts  1.89 us

profile of v2, /device:TPU:0, one launch (start us, length us, event | category | flops | bytes accessed | tf_op | source)
XLA Modules:
  0.0 42.5 jit_solution(3638672746828087130)
XLA Ops:
  0.0 40.7 %shard_map.73 = f32[4,2,16,1024]{3,2,1,0:T(8,128)} custom-call(f32[128,16,512]{2,1,0:T(8,128)} %src.1, bf16[1,128,256]{2,1,0:T(8,128)(2,1)} %constant.6.clone.tx_in, bf16[128,256]{1,0:T(8,128)(2,1)} %constant.7.clone.ty_in, f32[192,1024]{1,0:T(8,128)} %constant.8.clone.rest_0_, f32[128]{0:T(128)} %rest_1_.1, f32[128]{0:T(128)} %rest_2_.1, f32[1,2048]{1,0:T(1,128)} %bitcast.3), custom_call_target="tpu_custom_call" | custom-call | tf_op jit(solution)/shard_map/pallas_call | solution.py:342
  40.7 1.9 %copy.9 = f32[8,16,1024]{2,1,0:T(8,128)} copy(f32[8,16,1024]{2,1,0:T(8,128)} %bitcast.2) | data formatting | bytes 1048576

commit v3 on v2

--- a/solution.py
+++ b/solution.py
@@ -13,6 +13,8 @@
 TILE = 256
 SUB = 8
 ROWS = 64
+MOST = 67043328
+SPARE = 14 << 20
 
 
 def angles(rows, modes, count):
@@ -66,9 +68,9 @@
     src, tx_in, ty_in, *rest,
 ):
     waves_in, sx_in, sy_in, sz_in, out = rest[:5]
-    tx, ty, waves, symbol_x, symbol_y, symbol_z = rest[5:11]
-    field, turned, send1, recv1, send2, recv2, send3, recv3, t_high, t_low, left_all, left = rest[11:23]
-    fs, ins, sent, r1, r2, r3 = rest[23:]
+    tx, ty, waves, symbol_z = rest[5:9]
+    field, turned, send1, recv1, send2, recv2, send3, recv3, t_high, t_low, left_all, left = rest[9:21]
+    symbol_x, symbol_y, fs, ins, sent, r1, r2, r3 = rest[21:]
 
     me_n, me_d = lax.axis_index("north"), lax.axis_index("deep")
     nx, ny_part, nz_part = src.shape
@@ -178,25 +180,30 @@
 
     coarse = waves.shape[0] // 2 - FINE
 
-    def table_step(a):
-        sin_a, cos_a = waves[pl.ds(a, 1), :], waves[pl.ds(coarse + a, 1), :]
-        table = sin_a * waves[2 * coarse + FINE :, :] + cos_a * waves[2 * coarse : 2 * coarse + FINE, :]
-        high, low = split(table)
-        at = pl.multiple_of(a * FINE, FINE)
-        t_high[pl.ds(at, FINE), :] = high
-        t_low[pl.ds(at, FINE), :] = low
-
-    loop(coarse, table_step)
-
-    def z_product(lhs, count, pair):
-        at = pl.multiple_of(pair * 2 * nz_part, 2 * nz_part)
-        for c in range(0, kept_z, TILE):
-            both = dot(lhs[: 2 * count], t_high[pl.ds(at, 2 * nz_part), c : c + TILE])
-            yield c, both[:count] + both[count:] + dot(
-                lhs[:count], t_low[pl.ds(at, 2 * nz_part), c : c + TILE]
-            )
-
-    def near_part(f, e):
+    def table_tile(c):
+        cols = slice(c, c + TILE)
+        cos_b = waves[2 * coarse + FINE :, cols]
+        sin_b = waves[2 * coarse : 2 * coarse + FINE, cols]
+
+        def table_step(g):
+            for k in range(4):
+                a = g * 4 + k
+                table = waves[pl.ds(a, 1), cols] * cos_b + waves[pl.ds(coarse + a, 1), cols] * sin_b
+                high, low = split(table)
+                at = pl.multiple_of(a * FINE, FINE)
+                t_high[pl.ds(at, FINE), cols] = high
+                t_low[pl.ds(at, FINE), cols] = low
+
+        loop(coarse // 4, table_step)
+
+    tiles = range(0, kept_z, TILE)
+
+    def z_tile(lhs, count, pair, c):
+        at = pl.ds(pl.multiple_of(pair * 2 * nz_part, 2 * nz_part), 2 * nz_part)
+        both = dot(lhs[: 2 * count], t_high[at, c : c + TILE])
+        return both[:count] + both[count:] + dot(lhs[:count], t_low[at, c : c + TILE])
+
+    def near_left(f, e):
         at = pl.ds(bases[f], half)
         block = recv1.at[e, lax.bitwise_xor(me_d, 1), :, at]
         pltpu.make_async_copy(block, block, r1.at[2 * each * halves + 1 + f * each + e]).wait()
@@ -206,10 +213,26 @@
             cols = pl.ds(pl.multiple_of(lax.rem(owner, 2) * nz_part, nz_part), nz_part)
             left_all[:count, cols] = high
             left_all[count:, cols] = low
-        for c, value in z_product(left_all, count, my_pair):
-            value = value.reshape(halves, half, SUB, TILE)
-            for h in range(halves):
-                send2[e, at, h * SUB : (h + 1) * SUB, c : c + TILE] = value[h]
+
+    def near_tile(f, e, c):
+        value = z_tile(left_all, halves * half * SUB, my_pair, c).reshape(halves, half, SUB, TILE)
+        for h in range(halves):
+            send2[e, pl.ds(bases[f], half), h * SUB : (h + 1) * SUB, c : c + TILE] = value[h]
+
+    def far_left(q, pair):
+        f, e, h, i, count = chunks[q]
+        at, rows = pl.ds(bases[f] + i, count), count * SUB
+        block = recv1.at[e, pl.ds(pair * 2, 2), h, at]
+        pltpu.make_async_copy(block, block, r1.at[q]).wait()
+        for k in range(2):
+            high, low = split(recv1[e, pair * 2 + k, h, at].reshape(rows, nz_part))
+            left[:rows, k * nz_part : (k + 1) * nz_part] = high
+            left[rows : 2 * rows, k * nz_part : (k + 1) * nz_part] = low
+
+    def far_tile(q, pair, c):
+        f, e, h, i, count = chunks[q]
+        value = z_tile(left, count * SUB, pair, c).reshape(count, SUB, TILE)
+        send2[e, pl.ds(bases[f] + i, count), h * SUB : (h + 1) * SUB, c : c + TILE] += value
 
     def inverse_roots():
         row = lax.broadcasted_iota(jnp.int32, (share_y, TILE), 0)
@@ -222,17 +245,12 @@
                 for c in range(0, kept_z, TILE):
                     out[d, e, :, c : c + TILE] = lax.rsqrt(part_x + part_y + symbol_z[:, c : c + TILE])
 
-    def units(e):
-        return parts if e == last else halves
-
-    def copy2(e, u, n):
-        rows = slice(None) if e == last else slice(u * SUB, (u + 1) * SUB)
-        cols = slice(u * TILE, (u + 1) * TILE) if e == last else slice(None)
+    def copy2(e, rows, cols, n):
         return pltpu.make_async_remote_copy(
             src_ref=send2.at[e, n, rows, cols],
             dst_ref=recv2.at[e, me_n, rows, cols],
             send_sem=sent.at[1],
-            recv_sem=r2.at[e + u if e == last else e],
+            recv_sem=r2.at[e + (cols.start // TILE if e == last else 0)],
             device_id={"north": n},
         )
 
@@ -243,15 +261,11 @@
         else:
             loop(count, body)
 
-    def send_north(f, e, u, i, count):
-        def one(k):
-            n = bases[f] + i + k
-            if f == 0:
-                copy2(e, u, n).start()
-            else:
-                pl.when(n != me_n)(lambda: copy2(e, u, n).start())
-
-        every(count, one)
+    def send_north(f, e, rows, cols, n):
+        if f == 0:
+            copy2(e, rows, cols, n).start()
+        else:
+            pl.when(n != me_n)(lambda: copy2(e, rows, cols, n).start())
 
     def copy3(e, p, r):
         to = lax.bitwise_xor(me_d, r)
@@ -276,29 +290,39 @@
         for r in (*range(2, deep), 1):
             copy3(e, p, r).start()
 
+    rivals = [lax.rem(my_pair + k, pairs) for k in range(1, pairs)]
+    whole = slice(0, kept_z)
     for q, (f, e, h, i, count) in enumerate(chunks):
-        if h == 0 and i == 0:
-            near_part(f, e)
-        rows = count * SUB
-        at = pl.ds(bases[f] + i, count)
-        for pair in range(1, pairs):
-            other = lax.rem(my_pair + pair, pairs)
-            block = recv1.at[e, pl.ds(other * 2, 2), h, at]
-            pltpu.make_async_copy(block, block, r1.at[q]).wait()
-            for k in range(2):
-                owner = other * 2 + k
-                high, low = split(recv1[e, owner, h, at].reshape(rows, nz_part))
-                left[:rows, k * nz_part : (k + 1) * nz_part] = high
-                left[rows : 2 * rows, k * nz_part : (k + 1) * nz_part] = low
-            for c, value in z_product(left, rows, other):
-                send2[e, at, h * SUB : (h + 1) * SUB, c : c + TILE] += value.reshape(count, SUB, TILE)
+        lines = slice(h * SUB, (h + 1) * SUB)
+        if q == 0:
+            for c in tiles:
+                table_tile(c)
+                if c == 0:
+                    near_left(f, e)
+                near_tile(f, e, c)
+                if len(rivals) == 1:
+                    if c == 0:
+                        far_left(q, rivals[0])
+                    far_tile(q, rivals[0], c)
+                    if e < last:
+                        every(count, lambda k: send_north(f, e, lines, slice(c, c + TILE), bases[f] + i + k))
+            inverse_roots()
+            if len(rivals) == 1:
+                continue
+        elif h == 0 and i == 0:
+            near_left(f, e)
+            for c in tiles:
+                near_tile(f, e, c)
+        for pair in rivals:
+            far_left(q, pair)
+            for c in tiles:
+                far_tile(q, pair, c)
         if e < last:
-            send_north(f, e, h, i, count)
+            every(count, lambda k: send_north(f, e, lines, whole, bases[f] + i + k))
         elif h == halves - 1:
-            for u in range(parts):
-                send_north(f, e, u, 0, half)
-        if q == 0:
-            inverse_roots()
+            order = sorted((u - (n == 0), n, u) for u in range(parts) for n in range(half))
+            for _, n, u in order:
+                send_north(f, e, slice(0, ny_part), slice(u * TILE, (u + 1) * TILE), bases[f] + n)
 
     for e in range(each):
         recv2[e, me_n] = send2[e, me_n]
@@ -339,28 +363,33 @@
     rows = SUB * north
     chunks = 2 * each * halves + 1
     operands = (source, tx, ty, waves, symbol_x, symbol_y, symbol_z[None, :])
+    buffers = [
+        *((t.shape, t.dtype) for t in (tx, ty, waves)),
+        ((1, nz), F32),
+        ((halves, nx, SUB, nz_part), F32),
+        ((SUB, 2 * nx, TILE), BF16),
+        ((each, deep, halves, north, SUB, nz_part), F32),
+        ((each, deep, halves, north, SUB, nz_part), F32),
+        ((each, north, ny_part, kept_z), F32),
+        ((each, north, ny_part, kept_z), F32),
+        ((each, deep, share_y, kept_z), F32),
+        ((deep, each, share_y, kept_z), F32),
+        ((nz, kept_z), BF16),
+        ((nz, kept_z), BF16),
+        ((halves * rows, 2 * nz_part), BF16),
+        ((rows, 2 * nz_part), BF16),
+    ]
+    used = sum(int(np.prod(shape)) * jnp.dtype(kind).itemsize for shape, kind in buffers)
+    limit = MOST - SPARE if used < MOST - 2 * SPARE else MOST
     v = pl.pallas_call(
         functools.partial(kernel, north, deep, each),
         out_shape=jax.ShapeDtypeStruct((deep, each, share_y, kept_z), F32),
         in_specs=[remote] * len(operands),
         out_specs=pl.BlockSpec(memory_space=pltpu.VMEM),
-        scratch_shapes=[pltpu.VMEM(t.shape, t.dtype) for t in (tx, ty, waves)]
+        scratch_shapes=[pltpu.VMEM(shape, kind) for shape, kind in buffers]
         + [
             pltpu.SMEM(symbol_x.shape, F32),
             pltpu.SMEM(symbol_y.shape, F32),
-            pltpu.VMEM((1, nz), F32),
-            pltpu.VMEM((halves, nx, SUB, nz_part), F32),
-            pltpu.VMEM((SUB, 2 * nx, TILE), BF16),
-            pltpu.VMEM((each, deep, halves, north, SUB, nz_part), F32),
-            pltpu.VMEM((each, deep, halves, north, SUB, nz_part), F32),
-            pltpu.VMEM((each, north, ny_part, kept_z), F32),
-            pltpu.VMEM((each, north, ny_part, kept_z), F32),
-            pltpu.VMEM((each, deep, share_y, kept_z), F32),
-            pltpu.VMEM((deep, each, share_y, kept_z), F32),
-            pltpu.VMEM((nz, kept_z), BF16),
-            pltpu.VMEM((nz, kept_z), BF16),
-            pltpu.VMEM((halves * rows, 2 * nz_part), BF16),
-            pltpu.VMEM((rows, 2 * nz_part), BF16),
             pltpu.SemaphoreType.DMA((halves * nz_part // TILE,)),
             pltpu.SemaphoreType.DMA((len(operands) - 1,)),
         ]
@@ -369,9 +398,9 @@
             for count in (3, chunks + 2 * each, each + kept_z // TILE, each + kept_z // TILE)
         ],
         compiler_params=pltpu.CompilerParams(
-            collective_id=0, has_side_effects=True, vmem_limit_bytes=67043328
+            collective_id=0, has_side_effects=True, vmem_limit_bytes=limit
         ),
-    )(*operands)
+    )(*(pltpu.with_memory_space_constraint(operand, pltpu.HBM) for operand in operands))
     return v.reshape(deep * each, share_y, kept_z)
 
 

time: 42.7 us -> 40.7 us (0.953)
  local copies, waits for them, and re-layouts: 1.89 us -> 0.8 us
  Pallas kernels: 40.7 us -> 39.7 us
    unnamed x1, local copies, waits for them, and re-layouts: 1.89 us -> 0.8 us
    pallas_call x1, Pallas kernels: 40.7 us -> 39.7 us  [on_device(): pl.pallas_call(functools.partial(kernel, north, deep, each), out_shape=ja...]
where the time goes in v3:
time: 40.7 us; the launch traced here: 40.6 us
  Pallas kernels  39.7 us (98%)
  local copies, waits for them, and re-layouts  0.8 us (2%)
    pallas_call x1, Pallas kernels, on_device(): pl.pallas_call(functools.partial(kernel, north, deep, each), out_shape=ja...  39.7 us

profile of v3, /device:TPU:0, one launch (start us, length us, event | category | flops | bytes accessed | tf_op | source)
XLA Modules:
  0.0 40.6 jit_solution(5746503930562793152)
XLA Ops:
  0.0 39.7 %shard_map.73 = f32[4,2,16,1024]{3,2,1,0:T(8,128)S(1)} custom-call(f32[128,16,512]{2,1,0:T(8,128)} %src.1, bf16[1,128,256]{2,1,0:T(8,128)(2,1)} %constant.6.clone.tx_in, bf16[128,256]{1,0:T(8,128)(2,1)} %constant.7.clone.ty_in, f32[192,1024]{1,0:T(8,128)} %constant.8.clone.rest_0_, f32[128]{0:T(128)} %rest_1_.1, f32[128]{0:T(128)} %rest_2_.1, f32[1,2048]{1,0:T(1,128)} %bitcast.3), custom_call_target="tpu_custom_call" | custom-call | tf_op jit(solution)/shard_map/pallas_call | solution.py:384
  39.8 0.8 %copy.9 = f32[8,16,1024]{2,1,0:T(8,128)} copy(f32[8,16,1024]{2,1,0:T(8,128)S(1)} %bitcast.2) | data formatting | bytes 1048576

commit v4 on v3

--- a/solution.py
+++ b/solution.py
@@ -11,6 +11,7 @@
 F32, BF16 = jnp.float32, jnp.bfloat16
 FINE = 32
 TILE = 256
+WIDE = 512
 SUB = 8
 ROWS = 64
 MOST = 67043328
@@ -267,6 +268,9 @@
         else:
             pl.when(n != me_n)(lambda: copy2(e, rows, cols, n).start())
 
+    def send_slice(f, u, n):
+        send_north(f, last, slice(0, ny_part), slice(u * TILE, (u + 1) * TILE), bases[f] + n)
+
     def copy3(e, p, r):
         to = lax.bitwise_xor(me_d, r)
         cols = slice(p * TILE, (p + 1) * TILE) if e == last else slice(None)
@@ -290,22 +294,27 @@
         for r in (*range(2, deep), 1):
             copy3(e, p, r).start()
 
+    far_chunks = sum(chunk[0] == 0 for chunk in chunks)
     rivals = [lax.rem(my_pair + k, pairs) for k in range(1, pairs)]
     whole = slice(0, kept_z)
     for q, (f, e, h, i, count) in enumerate(chunks):
         lines = slice(h * SUB, (h + 1) * SUB)
         if q == 0:
-            for c in tiles:
-                table_tile(c)
-                if c == 0:
+            for c0 in range(0, kept_z, WIDE):
+                wide = range(c0, c0 + WIDE, TILE)
+                for c in wide:
+                    table_tile(c)
+                if c0 == 0:
                     near_left(f, e)
-                near_tile(f, e, c)
+                for c in wide:
+                    near_tile(f, e, c)
                 if len(rivals) == 1:
-                    if c == 0:
+                    if c0 == 0:
                         far_left(q, rivals[0])
-                    far_tile(q, rivals[0], c)
+                    for c in wide:
+                        far_tile(q, rivals[0], c)
                     if e < last:
-                        every(count, lambda k: send_north(f, e, lines, slice(c, c + TILE), bases[f] + i + k))
+                        every(count, lambda k: send_north(f, e, lines, slice(c0, c0 + WIDE), bases[f] + i + k))
             inverse_roots()
             if len(rivals) == 1:
                 continue
@@ -320,9 +329,16 @@
         if e < last:
             every(count, lambda k: send_north(f, e, lines, whole, bases[f] + i + k))
         elif h == halves - 1:
-            order = sorted((u - (n == 0), n, u) for u in range(parts) for n in range(half))
-            for _, n, u in order:
-                send_north(f, e, slice(0, ny_part), slice(u * TILE, (u + 1) * TILE), bases[f] + n)
+            for u in range(parts) if f else range(2):
+                every(half, lambda n: send_slice(f, u, n))
+        if f and each > 1:
+            u = q - far_chunks + 2
+            if u < parts:
+                every(half - 1, lambda n: send_slice(0, u, n + 1))
+        if q + 1 >= far_chunks and each > 1:
+            u = q - far_chunks + 3
+            if u < parts:
+                send_slice(0, u, 0)
 
     for e in range(each):
         recv2[e, me_n] = send2[e, me_n]

time: 40.7 us -> 40.6 us (level)
  no operation moved by 1% of the time
where the time goes in v4:
time: 40.6 us; the launch traced here: 40.5 us
  Pallas kernels  39.7 us (98%)
  local copies, waits for them, and re-layouts  0.8 us (2%)
    pallas_call x1, Pallas kernels, on_device(): pl.pallas_call(functools.partial(kernel, north, deep, each), out_shape=ja...  39.7 us

profile of v4, /device:TPU:0, one launch (start us, length us, event | category | flops | bytes accessed | tf_op | source)
XLA Modules:
  0.0 40.5 jit_solution(11695830071822069728)
XLA Ops:
  0.0 39.7 %shard_map.73 = f32[4,2,16,1024]{3,2,1,0:T(8,128)S(1)} custom-call(f32[128,16,512]{2,1,0:T(8,128)} %src.1, bf16[1,128,256]{2,1,0:T(8,128)(2,1)} %constant.6.clone.tx_in, bf16[128,256]{1,0:T(8,128)(2,1)} %constant.7.clone.ty_in, f32[192,1024]{1,0:T(8,128)} %constant.8.clone.rest_0_, f32[128]{0:T(128)} %rest_1_.1, f32[128]{0:T(128)} %rest_2_.1, f32[1,2048]{1,0:T(1,128)} %bitcast.3), custom_call_target="tpu_custom_call" | custom-call | tf_op jit(solution)/shard_map/pallas_call | solution.py:400
  39.7 0.8 %copy.9 = f32[8,16,1024]{2,1,0:T(8,128)} copy(f32[8,16,1024]{2,1,0:T(8,128)S(1)} %bitcast.2) | data formatting | bytes 1048576

commit v5 on v4

--- a/solution.py
+++ b/solution.py
@@ -268,8 +268,8 @@
         else:
             pl.when(n != me_n)(lambda: copy2(e, rows, cols, n).start())
 
-    def send_slice(f, u, n):
-        send_north(f, last, slice(0, ny_part), slice(u * TILE, (u + 1) * TILE), bases[f] + n)
+    def send_slice(f, rows, u, n):
+        send_north(f, last, rows, slice(u * TILE, (u + 1) * TILE), bases[f] + n)
 
     def copy3(e, p, r):
         to = lax.bitwise_xor(me_d, r)
@@ -328,23 +328,24 @@
                 far_tile(q, pair, c)
         if e < last:
             every(count, lambda k: send_north(f, e, lines, whole, bases[f] + i + k))
-        elif h == halves - 1:
-            for u in range(parts) if f else range(2):
-                every(half, lambda n: send_slice(f, u, n))
-        if f and each > 1:
-            u = q - far_chunks + 2
-            if u < parts:
-                every(half - 1, lambda n: send_slice(0, u, n + 1))
-        if q + 1 >= far_chunks and each > 1:
-            u = q - far_chunks + 3
-            if u < parts:
-                send_slice(0, u, 0)
-
-    for e in range(each):
-        recv2[e, me_n] = send2[e, me_n]
-    for e in range(each):
-        for p in range(parts if e == last else 1):
-            y_stage(e, p)
+        elif f:
+            for u in range(parts):
+                every(half, lambda n: send_slice(f, lines, u, n))
+        if far_chunks - 1 <= q < far_chunks + parts - 1:
+            u = q - far_chunks + 1
+            for n in range(half):
+                v = u + (n < half // 2)
+                for v in range(v + 1) if u == 0 else (v,):
+                    if v < parts:
+                        send_slice(0, slice(0, ny_part), v, n)
+        if f and h == halves - 1:
+            recv2[e, me_n] = send2[e, me_n]
+        if q == len(chunks) - 2:
+            for k in range(last):
+                y_stage(k, 0)
+
+    for p in range(parts):
+        y_stage(last, p)
 
     for e in range(each):
         out[me_d, e] = out[me_d, e] * send3[e, me_d]

time: 40.6 us -> 40.7 us (level)
  no operation moved by 1% of the time
where the time goes in v5:
time: 40.7 us; the launch traced here: 40.6 us
  Pallas kernels  39.8 us (98%)
  local copies, waits for them, and re-layouts  0.8 us (2%)
    pallas_call x1, Pallas kernels, on_device(): pl.pallas_call(functools.partial(kernel, north, deep, each), out_shape=ja...  39.8 us

profile of v5, /device:TPU:0, one launch (start us, length us, event | category | flops | bytes accessed | tf_op | source)
XLA Modules:
  0.0 40.6 jit_solution(18111982536602097117)
XLA Ops:
  0.0 39.8 %shard_map.73 = f32[4,2,16,1024]{3,2,1,0:T(8,128)S(1)} custom-call(f32[128,16,512]{2,1,0:T(8,128)} %src.1, bf16[1,128,256]{2,1,0:T(8,128)(2,1)} %constant.6.clone.tx_in, bf16[128,256]{1,0:T(8,128)(2,1)} %constant.7.clone.ty_in, f32[192,1024]{1,0:T(8,128)} %constant.8.clone.rest_0_, f32[128]{0:T(128)} %rest_1_.1, f32[128]{0:T(128)} %rest_2_.1, f32[1,2048]{1,0:T(1,128)} %bitcast.3), custom_call_target="tpu_custom_call" | custom-call | tf_op jit(solution)/shard_map/pallas_call | solution.py:401
  39.8 0.8 %copy.9 = f32[8,16,1024]{2,1,0:T(8,128)} copy(f32[8,16,1024]{2,1,0:T(8,128)S(1)} %bitcast.2) | data formatting | bytes 1048576

commit v6 on v5

--- a/solution.py
+++ b/solution.py
@@ -143,15 +143,19 @@
     chunks = []
     for f in range(2):
         for e in range(each):
+            if f and e == last:
+                cut = half // 2
+                chunks += [(f, e, 0, halves, i, cut) for i in range(0, half, cut)]
+                continue
             for h in range(halves):
-                cut = half // 2 if not chunks and half % 2 == 0 else half
-                chunks += [(f, e, h, i, cut) for i in range(0, half, cut)]
+                cut = half if chunks else half // 2
+                chunks += [(f, e, h, 1, i, cut) for i in range(0, half, cut)]
 
     def copy1(q, r):
-        f, e, h, i, count = chunks[q]
-        at = pl.ds(bases[f] + i, count)
+        f, e, h, hs, i, count = chunks[q]
+        at, h = pl.ds(bases[f] + i, count), pl.ds(h, hs)
         to = lax.bitwise_xor(me_d, r)
-        key = 2 * each * halves + 1 + f * each + e if r == 1 else q
+        key = len(chunks) + f * each + e if r == 1 else q
         return pltpu.make_async_remote_copy(
             src_ref=send1.at[e, to, h, at],
             dst_ref=recv1.at[e, me_d, h, at],
@@ -162,7 +166,7 @@
 
     def send_modes(h_done):
         for q, chunk in enumerate(chunks):
-            if (q < half // chunks[0][4]) == (h_done == 0):
+            if (q < 2) == (h_done == 0):
                 for r in (*range(2, deep), 1):
                     copy1(q, r).start()
 
@@ -207,7 +211,7 @@
     def near_left(f, e):
         at = pl.ds(bases[f], half)
         block = recv1.at[e, lax.bitwise_xor(me_d, 1), :, at]
-        pltpu.make_async_copy(block, block, r1.at[2 * each * halves + 1 + f * each + e]).wait()
+        pltpu.make_async_copy(block, block, r1.at[len(chunks) + f * each + e]).wait()
         count = halves * half * SUB
         for owner, block in ((me_d, send1), (lax.bitwise_xor(me_d, 1), recv1)):
             high, low = split(block[e, owner, :, at].reshape(count, nz_part))
@@ -221,8 +225,8 @@
             send2[e, pl.ds(bases[f], half), h * SUB : (h + 1) * SUB, c : c + TILE] = value[h]
 
     def far_left(q, pair):
-        f, e, h, i, count = chunks[q]
-        at, rows = pl.ds(bases[f] + i, count), count * SUB
+        f, e, h, hs, i, count = chunks[q]
+        at, rows, h = pl.ds(bases[f] + i, count), hs * count * SUB, pl.ds(h, hs)
         block = recv1.at[e, pl.ds(pair * 2, 2), h, at]
         pltpu.make_async_copy(block, block, r1.at[q]).wait()
         for k in range(2):
@@ -231,9 +235,11 @@
             left[rows : 2 * rows, k * nz_part : (k + 1) * nz_part] = low
 
     def far_tile(q, pair, c):
-        f, e, h, i, count = chunks[q]
-        value = z_tile(left, count * SUB, pair, c).reshape(count, SUB, TILE)
-        send2[e, pl.ds(bases[f] + i, count), h * SUB : (h + 1) * SUB, c : c + TILE] += value
+        f, e, h, hs, i, count = chunks[q]
+        value = z_tile(left, hs * count * SUB, pair, c).reshape(hs, count, SUB, TILE)
+        for k in range(hs):
+            rows = slice((h + k) * SUB, (h + k + 1) * SUB)
+            send2[e, pl.ds(bases[f] + i, count), rows, c : c + TILE] += value[k]
 
     def inverse_roots():
         row = lax.broadcasted_iota(jnp.int32, (share_y, TILE), 0)
@@ -297,8 +303,8 @@
     far_chunks = sum(chunk[0] == 0 for chunk in chunks)
     rivals = [lax.rem(my_pair + k, pairs) for k in range(1, pairs)]
     whole = slice(0, kept_z)
-    for q, (f, e, h, i, count) in enumerate(chunks):
-        lines = slice(h * SUB, (h + 1) * SUB)
+    for q, (f, e, h, hs, i, count) in enumerate(chunks):
+        lines = slice(h * SUB, (h + hs) * SUB)
         if q == 0:
             for c0 in range(0, kept_z, WIDE):
                 wide = range(c0, c0 + WIDE, TILE)
@@ -330,15 +336,13 @@
             every(count, lambda k: send_north(f, e, lines, whole, bases[f] + i + k))
         elif f:
             for u in range(parts):
-                every(half, lambda n: send_slice(f, lines, u, n))
-        if far_chunks - 1 <= q < far_chunks + parts - 1:
-            u = q - far_chunks + 1
-            for n in range(half):
-                v = u + (n < half // 2)
-                for v in range(v + 1) if u == 0 else (v,):
-                    if v < parts:
-                        send_slice(0, slice(0, ny_part), v, n)
-        if f and h == halves - 1:
+                every(count, lambda n: send_slice(f, lines, u, i + n))
+        u = q - far_chunks + 1
+        if 0 <= u < parts - 1:
+            every(half, lambda n: send_slice(0, slice(0, ny_part), u, n))
+        elif parts - 1 <= u <= parts:
+            every(half // 2, lambda n: send_slice(0, slice(0, ny_part), parts - 1, n + (u == parts) * (half // 2)))
+        if f and h + hs == halves and i + count == half:
             recv2[e, me_n] = send2[e, me_n]
         if q == len(chunks) - 2:
             for k in range(last):
@@ -378,7 +382,7 @@
     waves = long_tables(nz)
     remote = pl.BlockSpec(memory_space=pltpu.HBM)
     rows = SUB * north
-    chunks = 2 * each * halves + 1
+    chunks = 2 * each * halves + 3 - halves
     operands = (source, tx, ty, waves, symbol_x, symbol_y, symbol_z[None, :])
     buffers = [
         *((t.shape, t.dtype) for t in (tx, ty, waves)),

time: 40.7 us -> 39 us (0.958)
  Pallas kernels: 39.8 us -> 38 us
    pallas_call x1, Pallas kernels: 39.8 us -> 38 us  [on_device(): pl.pallas_call(functools.partial(kernel, north, deep, each), out_shape=ja...]
where the time goes in v6:
time: 39 us; the launch traced here: 38.8 us
  Pallas kernels  38 us (97%)
  local copies, waits for them, and re-layouts  0.8 us (2%)
    pallas_call x1, Pallas kernels, on_device(): pl.pallas_call(functools.partial(kernel, north, deep, each), out_shape=ja...  38 us
    unnamed x1, local copies, waits for them, and re-layouts  0.8 us

profile of v6, /device:TPU:0, one launch (start us, length us, event | category | flops | bytes accessed | tf_op | source)
XLA Modules:
  0.0 38.8 jit_solution(13921842338008151135)
XLA Ops:
  0.0 38.0 %shard_map.73 = f32[4,2,16,1024]{3,2,1,0:T(8,128)S(1)} custom-call(f32[128,16,512]{2,1,0:T(8,128)} %src.1, bf16[1,128,256]{2,1,0:T(8,128)(2,1)} %constant.6.clone.tx_in, bf16[128,256]{1,0:T(8,128)(2,1)} %constant.7.clone.ty_in, f32[192,1024]{1,0:T(8,128)} %constant.8.clone.rest_0_, f32[128]{0:T(128)} %rest_1_.1, f32[128]{0:T(128)} %rest_2_.1, f32[1,2048]{1,0:T(1,128)} %bitcast.3), custom_call_target="tpu_custom_call" | custom-call | tf_op jit(solution)/shard_map/pallas_call | solution.py:405
  38.0 0.8 %copy.9 = f32[8,16,1024]{2,1,0:T(8,128)} copy(f32[8,16,1024]{2,1,0:T(8,128)S(1)} %bitcast.2) | data formatting | bytes 1048576

commit v7 on v6

--- a/solution.py
+++ b/solution.py
@@ -141,19 +141,22 @@
         loop(tx.shape[0], modes_of)
 
     chunks = []
-    for f in range(2):
-        for e in range(each):
-            if f and e == last:
-                cut = half // 2
-                chunks += [(f, e, 0, halves, i, cut) for i in range(0, half, cut)]
-                continue
-            for h in range(halves):
-                cut = half if chunks else half // 2
-                chunks += [(f, e, h, 1, i, cut) for i in range(0, half, cut)]
+    for e in range(each):
+        for h in range(halves):
+            cut = half if chunks else half // 2
+            chunks += [(0, e, h, 1, i, cut) for i in range(0, half, cut)]
+    for e in range(each):
+        chunks += [(1, e, 0, halves, i, half // 2) for i in range(0, half, half // 2)]
+
+    def start_of(q):
+        f, e, _, _, i, count = chunks[q]
+        if f and e < last:
+            i = jnp.where(me_n < half, i, half - count - i)
+        return bases[f] + i
 
     def copy1(q, r):
         f, e, h, hs, i, count = chunks[q]
-        at, h = pl.ds(bases[f] + i, count), pl.ds(h, hs)
+        at, h = pl.ds(start_of(q), count), pl.ds(h, hs)
         to = lax.bitwise_xor(me_d, r)
         key = len(chunks) + f * each + e if r == 1 else q
         return pltpu.make_async_remote_copy(
@@ -226,7 +229,7 @@
 
     def far_left(q, pair):
         f, e, h, hs, i, count = chunks[q]
-        at, rows, h = pl.ds(bases[f] + i, count), hs * count * SUB, pl.ds(h, hs)
+        at, rows, h = pl.ds(start_of(q), count), hs * count * SUB, pl.ds(h, hs)
         block = recv1.at[e, pl.ds(pair * 2, 2), h, at]
         pltpu.make_async_copy(block, block, r1.at[q]).wait()
         for k in range(2):
@@ -239,7 +242,7 @@
         value = z_tile(left, hs * count * SUB, pair, c).reshape(hs, count, SUB, TILE)
         for k in range(hs):
             rows = slice((h + k) * SUB, (h + k + 1) * SUB)
-            send2[e, pl.ds(bases[f] + i, count), rows, c : c + TILE] += value[k]
+            send2[e, pl.ds(start_of(q), count), rows, c : c + TILE] += value[k]
 
     def inverse_roots():
         row = lax.broadcasted_iota(jnp.int32, (share_y, TILE), 0)
@@ -300,6 +303,7 @@
         for r in (*range(2, deep), 1):
             copy3(e, p, r).start()
 
+    remote = jnp.where(me_n < half, half // 2, 0)
     far_chunks = sum(chunk[0] == 0 for chunk in chunks)
     rivals = [lax.rem(my_pair + k, pairs) for k in range(1, pairs)]
     whole = slice(0, kept_z)
@@ -333,20 +337,23 @@
             for c in tiles:
                 far_tile(q, pair, c)
         if e < last:
-            every(count, lambda k: send_north(f, e, lines, whole, bases[f] + i + k))
+            every(count, lambda k: send_north(f, e, lines, whole, start_of(q) + k))
         elif f:
             for u in range(parts):
                 every(count, lambda n: send_slice(f, lines, u, i + n))
         u = q - far_chunks + 1
-        if 0 <= u < parts - 1:
-            every(half, lambda n: send_slice(0, slice(0, ny_part), u, n))
-        elif parts - 1 <= u <= parts:
-            every(half // 2, lambda n: send_slice(0, slice(0, ny_part), parts - 1, n + (u == parts) * (half // 2)))
-        if f and h + hs == halves and i + count == half:
+        for v in {0: (0, 1)}.get(u, (u + 1,)) if 0 <= u < parts - 1 else ():
+            every(half // 2, lambda n: send_slice(0, slice(0, ny_part), v, remote + n))
+        if 0 <= u < parts:
+            every(half // 2, lambda n: send_slice(0, slice(0, ny_part), u, half // 2 - remote + n))
+        if f and i + count == half:
             recv2[e, me_n] = send2[e, me_n]
-        if q == len(chunks) - 2:
-            for k in range(last):
-                y_stage(k, 0)
+        if q >= len(chunks) - 2:
+            @pl.when(lax.rem(me_n, half) // (half // 2) == q - len(chunks) + 2)
+            def _():
+                for k in range(last):
+                    y_stage(k, 0)
+
 
     for p in range(parts):
         y_stage(last, p)
@@ -382,7 +389,7 @@
     waves = long_tables(nz)
     remote = pl.BlockSpec(memory_space=pltpu.HBM)
     rows = SUB * north
-    chunks = 2 * each * halves + 3 - halves
+    chunks = each * halves + 1 + 2 * each
     operands = (source, tx, ty, waves, symbol_x, symbol_y, symbol_z[None, :])
     buffers = [
         *((t.shape, t.dtype) for t in (tx, ty, waves)),

time: 39 us -> 38.6 us (0.990)
  Pallas kernels: 38 us -> 37.3 us
    pallas_call x1, Pallas kernels: 38 us -> 37.3 us  [on_device(): pl.pallas_call(functools.partial(kernel, north, deep, each), out_shape=ja...]
where the time goes in v7:
time: 38.6 us; the launch traced here: 38.2 us
  Pallas kernels  37.3 us (97%)
  local copies, waits for them, and re-layouts  0.8 us (2%)
    pallas_call x1, Pallas kernels, on_device(): pl.pallas_call(functools.partial(kernel, north, deep, each), out_shape=ja...  37.3 us
    unnamed x1, local copies, waits for them, and re-layouts  0.8 us

profile of v7, /device:TPU:0, one launch (start us, length us, event | category | flops | bytes accessed | tf_op | source)
XLA Modules:
  0.0 38.2 jit_solution(8773722801152085750)
XLA Ops:
  0.0 37.3 %shard_map.73 = f32[4,2,16,1024]{3,2,1,0:T(8,128)S(1)} custom-call(f32[128,16,512]{2,1,0:T(8,128)} %src.1, bf16[1,128,256]{2,1,0:T(8,128)(2,1)} %constant.6.clone.tx_in, bf16[128,256]{1,0:T(8,128)(2,1)} %constant.7.clone.ty_in, f32[192,1024]{1,0:T(8,128)} %constant.8.clone.rest_0_, f32[128]{0:T(128)} %rest_1_.1, f32[128]{0:T(128)} %rest_2_.1, f32[1,2048]{1,0:T(1,128)} %bitcast.3), custom_call_target="tpu_custom_call" | custom-call | tf_op jit(solution)/shard_map/pallas_call | solution.py:412
  37.4 0.8 %copy.9 = f32[8,16,1024]{2,1,0:T(8,128)} copy(f32[8,16,1024]{2,1,0:T(8,128)S(1)} %bitcast.2) | data formatting | bytes 1048576

commit v8 on v7

--- a/solution.py
+++ b/solution.py
@@ -146,12 +146,22 @@
             cut = half if chunks else half // 2
             chunks += [(0, e, h, 1, i, cut) for i in range(0, half, cut)]
     for e in range(each):
-        chunks += [(1, e, 0, halves, i, half // 2) for i in range(0, half, half // 2)]
+        cut = half // 2 if e < last else 1
+        chunks += [(1, e, 0, halves, i, cut) for i in range(0, half, cut)]
+
+    first_pair = lax.rem(me_n, half) < half // 2
 
     def start_of(q):
         f, e, _, _, i, count = chunks[q]
         if f and e < last:
             i = jnp.where(me_n < half, i, half - count - i)
+        elif f:
+            rank = lax.rem(me_n, half)
+            turns = [lax.bitwise_xor(rank, k) for k in range(half)]
+            if half == 4:
+                i = jnp.where(first_pair, (turns[1], 2, 3, rank)[i], (0, 1, turns[1], rank)[i])
+            else:
+                i = turns[(i + 1) % half]
         return bases[f] + i
 
     def copy1(q, r):
@@ -338,9 +348,9 @@
                 far_tile(q, pair, c)
         if e < last:
             every(count, lambda k: send_north(f, e, lines, whole, start_of(q) + k))
-        elif f:
+        elif f and i + 1 < half:
             for u in range(parts):
-                every(count, lambda n: send_slice(f, lines, u, i + n))
+                copy2(e, lines, slice(u * TILE, (u + 1) * TILE), start_of(q)).start()
         u = q - far_chunks + 1
         for v in {0: (0, 1)}.get(u, (u + 1,)) if 0 <= u < parts - 1 else ():
             every(half // 2, lambda n: send_slice(0, slice(0, ny_part), v, remote + n))
@@ -348,8 +358,8 @@
             every(half // 2, lambda n: send_slice(0, slice(0, ny_part), u, half // 2 - remote + n))
         if f and i + count == half:
             recv2[e, me_n] = send2[e, me_n]
-        if q >= len(chunks) - 2:
-            @pl.when(lax.rem(me_n, half) // (half // 2) == q - len(chunks) + 2)
+        if q in (len(chunks) - 3, len(chunks) - 1):
+            @pl.when(first_pair if q < len(chunks) - 1 else jnp.logical_not(first_pair))
             def _():
                 for k in range(last):
                     y_stage(k, 0)
@@ -389,7 +399,7 @@
     waves = long_tables(nz)
     remote = pl.BlockSpec(memory_space=pltpu.HBM)
     rows = SUB * north
-    chunks = each * halves + 1 + 2 * each
+    chunks = each * halves + 1 + 2 * (each - 1) + north // 2
     operands = (source, tx, ty, waves, symbol_x, symbol_y, symbol_z[None, :])
     buffers = [
         *((t.shape, t.dtype) for t in (tx, ty, waves)),

time: 38.6 us -> 38.4 us (level)
  Pallas kernels: 37.3 us -> 36.9 us
    pallas_call x1, Pallas kernels: 37.3 us -> 36.9 us  [on_device(): pl.pallas_call(functools.partial(kernel, north, deep, each), out_shape=ja...]
where the time goes in v8:
time: 38.4 us; the launch traced here: 37.7 us
  Pallas kernels  36.9 us (96%)
  local copies, waits for them, and re-layouts  0.8 us (2%)
    pallas_call x1, Pallas kernels, on_device(): pl.pallas_call(functools.partial(kernel, north, deep, each), out_shape=ja...  36.9 us
    unnamed x1, local copies, waits for them, and re-layouts  0.8 us

profile of v8, /device:TPU:0, one launch (start us, length us, event | category | flops | bytes accessed | tf_op | source)
XLA Modules:
  0.0 37.7 jit_solution(6693968187802965739)
XLA Ops:
  0.0 36.9 %shard_map.73 = f32[4,2,16,1024]{3,2,1,0:T(8,128)S(1)} custom-call(f32[128,16,512]{2,1,0:T(8,128)} %src.1, bf16[1,128,256]{2,1,0:T(8,128)(2,1)} %constant.6.clone.tx_in, bf16[128,256]{1,0:T(8,128)(2,1)} %constant.7.clone.ty_in, f32[192,1024]{1,0:T(8,128)} %constant.8.clone.rest_0_, f32[128]{0:T(128)} %rest_1_.1, f32[128]{0:T(128)} %rest_2_.1, f32[1,2048]{1,0:T(1,128)} %bitcast.3), custom_call_target="tpu_custom_call" | custom-call | tf_op jit(solution)/shard_map/pallas_call | solution.py:422
  36.9 0.8 %copy.9 = f32[8,16,1024]{2,1,0:T(8,128)} copy(f32[8,16,1024]{2,1,0:T(8,128)S(1)} %bitcast.2) | data formatting | bytes 1048576
